TPU v7x, 128 devices: a whole 4x4x4 slice. The times are simulated.
128 devices in a mesh: gx: 4 (over x_hi, core), gy: 4 (over y), gz: 8 (over z, x_lo).
Axes of the slice: x: 4 (x_hi: 2, x_lo: 2; x = x_hi * 2 + x_lo), y: 4, z: 4, core: 2. Of those that a mesh axis runs over, the one named last changes fastest.
Arguments:
- field: float32 [64, 1024, 1024], P('gx', 'gy', 'gz'), may hold values from -6 to 6
- source: float32 [64, 1024, 1024], P('gx', 'gy', 'gz'), may hold values from -6 to 6
Outputs:
- smoothed: float32 [64, 1024, 1024], P('gx', 'gy', 'gz')
All inputs are finite; a program needn't handle non-finite values.
Results may differ from a plain program's by a relative error of at most 0.00002.
Values sent between devices are 32-bit elements; how exact they have to be, the bound alone decides.
A program may use at most 64 MiB of HBM per device.

v0:
```python
import functools
import itertools

import jax
import jax.numpy as jnp
from jax import lax
from jax.experimental import pallas as pl
from jax.experimental.pallas import tpu as pltpu
from jax.sharding import PartitionSpec as P

SWEEPS = 3
HALF = 2 * SWEEPS
PAD = 16
LANES = 128
CHUNK = 8
SIXTH = 1.0 / 6.0
MESH = pl.DeviceIdType.MESH
AXES = ("gx", "gy", "gz")
ROUTES = [r for r in itertools.product((-1, 0, 1), repeat=3) if 1 <= sum(map(abs, r)) <= 2]
f32 = jnp.float32
bf16 = jnp.bfloat16


def iota(shape, dim):
    return lax.broadcasted_iota(jnp.int32, shape, dim)


def side(step):
    return 0 if step < 0 else 1


def kernel(field, source, out, fbuf, sbuf, obuf, S, X, own, zout, zin, xzin, yzout, yzin,
           sown, szin, SC, C, U, Y, isem, osem, ssem, rsem):
    M = X.shape[1] - 2
    N = X.shape[2] - 2 * PAD
    T = N // 8
    H = M // 2
    at = {a: lax.axis_index(a) for a in AXES}
    size = {a: lax.axis_size(a) for a in AXES}
    has = (at["gx"] > 0, at["gx"] < size["gx"] - 1)

    def target(route):
        return {a: lax.rem(at[a] + step + size[a], size[a]) for a, step in zip(AXES, route) if step}

    def guarded(step, action):
        if step == 0:
            action()
        else:
            pl.when(has[side(step)])(action)

    rows = pl.ds(PAD, N)
    inner = pl.ds(1, M)
    first, last = pl.ds(PAD, 8), pl.ds(PAD + N - 8, 8)
    before, after = pl.ds(PAD - 8, 8), pl.ds(PAD + N, 8)
    edge_rows = ((first, after), (last, before))

    def refs(r, route):
        x, y, z = route
        h = 2 * r
        if x:
            src_plane, dst_plane = ((1, M + 1), (M, 0))[side(x)]
        if y:
            src_rows, dst_rows = edge_rows[side(y)]
        if x and y:
            return X.at[h, src_plane, src_rows], X.at[h, dst_plane, dst_rows]
        if x and z:
            return own.at[r, src_plane - 1], xzin.at[r, side(-x), side(-z)]
        if y and z:
            return yzout.at[r, side(y)], yzin.at[r, side(-y), side(-z)]
        if x:
            return X.at[h, src_plane, rows], X.at[h, dst_plane, rows]
        if y:
            return X.at[h, inner, src_rows], X.at[h, inner, dst_rows]
        return zout.at[r, side(z)], zin.at[r, side(-z)]

    def source_refs(route):
        x, y, z = route
        if x:
            src_plane, dst_plane = ((1, M + 1), (M, 0))[side(x)]
            return S.at[0, src_plane, rows], S.at[0, dst_plane, rows]
        if y:
            src_rows, dst_rows = edge_rows[side(y)]
            return S.at[0, inner, src_rows], S.at[0, inner, dst_rows]
        return sown, szin.at[side(-z)]

    def remote(r, route):
        pair = refs(r, route) if r < SWEEPS else source_refs(route)
        number = ROUTES.index(route)
        return pltpu.make_async_remote_copy(
            src_ref=pair[0], dst_ref=pair[1], send_sem=ssem.at[r, number], recv_sem=rsem.at[r, number],
            device_id=target(route), device_id_type=MESH)

    faces = [r for r in ROUTES if sum(map(abs, r)) == 1]

    def start(r, routes):
        for route in routes:
            guarded(route[0], lambda route=route: remote(r, route).start())

    def wait(r, routes):
        for route in routes:
            guarded(-route[0], lambda route=route: remote(r, route).wait_recv())

    planes = 2 * M // 4
    loads = []
    for slot, (big, small) in enumerate(((field, fbuf), (source, sbuf))):
        for part in (0, 3, 1, 2):
            here = pl.ds(part * planes, planes)
            loads.append(pltpu.make_async_copy(big.at[here], small.at[here], isem.at[slot, part]))
    for load in loads:
        load.start()
    barrier = pltpu.get_barrier_semaphore()
    count = jnp.int32(0)
    for route in ROUTES:
        guarded(route[0], lambda route=route: pl.semaphore_signal(
            barrier, inc=1, device_id=target(route), device_id_type=MESH))
        count = count + (1 if route[0] == 0 else has[side(route[0])].astype(jnp.int32))

    lane = iota((8, LANES), 1)
    sub = iota((8, LANES), 0)
    group = lane // 4
    place = lane % 4
    odd8 = (sub + lane) % 2 == 1
    outer = (lane == 0) | (lane == LANES - 1)
    odd_rows = (iota((8 * CHUNK, LANES), 0) + iota((8 * CHUNK, LANES), 1)) % 2 == 1
    outer_rows = (iota((8 * CHUNK, LANES), 1) == 0) | (iota((8 * CHUNK, LANES), 1) == LANES - 1)
    gap = jnp.abs(iota((LANES, LANES), 0) - iota((LANES, LANES), 1))
    beside_lanes = jnp.where(gap == 1, 1.0, 0.0).astype(bf16)
    beside_lanes = jnp.concatenate([beside_lanes, beside_lanes], 0)

    def turn(value, shift, axis=1):
        return pltpu.roll(value, shift % value.shape[axis], axis)

    def lane_sum(value):
        high = value.astype(bf16)
        rest = (value - high.astype(f32)).astype(bf16)
        return jnp.dot(jnp.concatenate([high, rest], 1), beside_lanes, preferred_element_type=f32)

    def swapped(value):
        where = iota(value.shape, 1) % 4
        return jnp.where(where == 1, turn(value, -1), turn(value, 1))

    def pack(acc, t, tile):
        return jnp.where(group == t, turn(tile, 4 * t + 2), acc)

    @pl.when(at["gx"] == 0)
    def _():
        for h in range(HALF):
            X[h, 0] = jnp.zeros(X.shape[2:], f32)
        for r in range(SWEEPS):
            xzin[r, 0] = jnp.zeros(xzin.shape[2:], f32)

    @pl.when(at["gx"] == size["gx"] - 1)
    def _():
        for h in range(HALF):
            X[h, M + 1] = jnp.zeros(X.shape[2:], f32)
        for r in range(SWEEPS):
            xzin[r, 1] = jnp.zeros(xzin.shape[2:], f32)

    def finish_pack(r):
        for m in range(H):
            one, two = own[r, m], own[r, m + H]
            zout[r, 0, m] = jnp.where(place >= 2, one, turn(two, -2))
            zout[r, 1, m] = jnp.where(place < 2, one, turn(two, 2))
        for m in range(M):
            yzout[r, 0, m:m + 1] = own[r, m, 0:1]
            yzout[r, 1, m:m + 1] = own[r, m, 7:8]

    order = [0, M - 1] + list(range(1, M - 1))
    x_routes = [r for r in ROUTES if r[0]]
    other_routes = [r for r in ROUTES if not r[0]]
    whole_odd = (iota((N, LANES), 0) + iota((N, LANES), 1)) % 2 == 1

    for load in loads[:4]:
        load.wait()
    for m in order:
        value = jnp.where(whole_odd, fbuf[2 * m], fbuf[2 * m + 1])
        X[0, m + 1, rows] = value
        acc = jnp.zeros((8, LANES), f32)
        for t in range(T):
            acc = pack(acc, t, value[8 * t:8 * t + 8])
        own[0, m] = acc
    finish_pack(0)
    pl.semaphore_wait(barrier, count)
    start(0, ROUTES)

    for load in loads[4:]:
        load.wait()
    for m in order:
        even_plane, odd_plane = sbuf[2 * m], sbuf[2 * m + 1]
        value = jnp.where(whole_odd, odd_plane, even_plane)
        S[0, m + 1, rows] = value
        S[1, m + 1, rows] = jnp.where(whole_odd, even_plane, odd_plane)
        acc = jnp.zeros((8, LANES), f32)
        for t in (range(T)):
            acc = pack(acc, t, value[8 * t:8 * t + 8])
        sown[m] = acc
    start(SWEEPS, faces)

    def update(h, m, start_row, length, wings, near=None):
        here = pl.ds(start_row, length)
        centre = X[h, m + 1, here]
        if near is None:
            low, high = X[h, m, here], X[h, m + 2, here]
            if h % 2:
                low, high = high, low
            near = jnp.where(odd_rows[:length], high, low)
        else:
            near = X[h, near + 1, here]
        total = (S[h % 2, m + 1, here] + centre) + (near + lane_sum(centre))
        total = total + (X[h, m + 1, pl.ds(start_row - 1, length)] + X[h, m + 1, pl.ds(start_row + 1, length)])
        return (total + jnp.where(outer_rows[:length], wings, 0.0)) * f32(SIXTH)

    def wings_of(edge, tiles):
        return jnp.concatenate([turn(edge, LANES - 2 - 4 * t) for t in tiles], 0)

    chunks = [range(c, min(c + CHUNK, T)) for c in range(0, T, CHUNK)]

    for r in range(SWEEPS):
        h = 2 * r
        wait(r, ROUTES)
        if r == 0:
            wait(SWEEPS, faces)
            for m in range(M):
                SC[m] = jnp.where(place == 1, szin[0, m], szin[1, m])
        for m in range(M):
            a, b = zin[r, 0, m % H], zin[r, 1, m % H]
            if m >= H:
                a, b = turn(a, -2), turn(b, 2)
            C[m + 1] = jnp.where(place == 1, a, b)
        C[0] = jnp.where(place == 1, xzin[r, 0, 0], xzin[r, 0, 1])
        C[M + 1] = jnp.where(place == 1, xzin[r, 1, 0], xzin[r, 1, 1])
        for m in range(M + 2):
            U[0, m] = swapped(C[m])
        small = (M, LANES)
        spot = iota(small, 1) % 4
        ends = (iota(small, 1) == 0) | (iota(small, 1) == LANES - 1)
        low_corner = jnp.where(spot == 1, yzin[r, 0, 0], yzin[r, 0, 1])
        high_corner = jnp.where(spot == 1, yzin[r, 1, 0], yzin[r, 1, 1])
        Y[0] = turn(low_corner, -4 * (T - 1))
        Y[1] = turn(high_corner, 4 * (T - 1))
        Y[2] = jnp.where(ends, turn(swapped(low_corner), LANES - 2 - 4 * (T - 1)), 0.0)
        Y[3] = jnp.where(ends, turn(swapped(high_corner), LANES - 2), 0.0)
        for m in range(M):
            a, b = zin[r, 0, m % H], zin[r, 1, m % H]
            if m >= H:
                a, b = turn(a, -2), turn(b, 2)
            mine = own[r, m]
            centre = C[m + 1]
            across = turn(jnp.where(place == 0, a, mine), 1) + turn(jnp.where(place == 3, b, mine), -1)
            above = turn(centre, -1, 0)
            above = jnp.where(sub == 7, turn(above, -4), above)
            above = jnp.where((sub == 7) & (group == T - 1), Y[1, m:m + 1], above)
            below = turn(centre, 1, 0)
            below = jnp.where(sub == 0, turn(below, 4), below)
            below = jnp.where((sub == 0) & (group == 0), Y[0, m:m + 1], below)
            near = jnp.where(odd8, C[m + 2], C[m])
            red = (SC[m] + centre + near + (across + (above + below))) * f32(SIXTH)
            U[1, m] = swapped(red)
        for m in range(M):
            for tiles in chunks:
                begin = PAD + 8 * tiles[0]
                value = update(h, m, begin, 8 * len(tiles), wings_of(U[0, m + 1], tiles))
                X[h + 1, m + 1, pl.ds(begin, 8 * len(tiles))] = value
            for k, begin in enumerate((PAD - 8, PAD + N)):
                X[h + 1, m + 1, pl.ds(begin, 8)] = update(
                    h, m, begin, 8, jnp.broadcast_to(Y[2 + k, m:m + 1], (8, LANES)))
        for k, (m, near) in enumerate(((-1, 0), (M, M - 1))):
            @pl.when(has[k])
            def _(m=m, near=near):
                for tiles in chunks:
                    begin = PAD + 8 * tiles[0]
                    X[h + 1, m + 1, pl.ds(begin, 8 * len(tiles))] = update(
                        h, m, begin, 8 * len(tiles), wings_of(U[0, m + 1], tiles), near)
        h += 1
        for number, m in enumerate(order):
            acc = jnp.zeros((8, LANES), f32)
            for tiles in chunks:
                begin, length = PAD + 8 * tiles[0], 8 * len(tiles)
                value = update(h, m, begin, length, wings_of(U[1, m], tiles))
                if r < SWEEPS - 1:
                    X[h + 1, m + 1, pl.ds(begin, length)] = value
                    for t in tiles:
                        acc = pack(acc, t, value[8 * (t - tiles[0]):8 * (t - tiles[0]) + 8])
                else:
                    red = X[h, m + 1, pl.ds(begin, length)]
                    obuf[2 * m, pl.ds(begin - PAD, length)] = jnp.where(odd_rows[:length], value, red)
                    obuf[2 * m + 1, pl.ds(begin - PAD, length)] = jnp.where(odd_rows[:length], red, value)
            if r < SWEEPS - 1:
                own[r + 1, m] = acc
                if number == 1:
                    start(r + 1, x_routes)
            else:
                pltpu.make_async_copy(obuf.at[pl.ds(2 * m, 2)], out.at[pl.ds(2 * m, 2)], osem.at[m]).start()
        if r < SWEEPS - 1:
            finish_pack(r + 1)
            start(r + 1, other_routes)

    for r in range(SWEEPS):
        for route in ROUTES:
            guarded(route[0], lambda route=route: remote(r, route).wait_send())
    for route in faces:
        guarded(route[0], lambda route=route: remote(SWEEPS, route).wait_send())
    for m in range(M):
        pltpu.make_async_copy(obuf.at[pl.ds(2 * m, 2)], out.at[pl.ds(2 * m, 2)], osem.at[m]).wait()


def on_device(field, source):
    L, N, K = field.shape
    M = L // 2
    vmem = lambda *shape: pltpu.VMEM(shape, f32)
    return pl.pallas_call(
        kernel,
        out_shape=jax.ShapeDtypeStruct(field.shape, f32),
        in_specs=[pl.BlockSpec(memory_space=pl.ANY)] * 2,
        out_specs=pl.BlockSpec(memory_space=pl.ANY),
        scratch_shapes=[
            vmem(L, N, K), vmem(L, N, K), vmem(L, N, K),
            vmem(2, M + 2, N + 2 * PAD, K),
            vmem(HALF, M + 2, N + 2 * PAD, K),
            vmem(SWEEPS, M, 8, K),
            vmem(SWEEPS, 2, M // 2, 8, K),
            vmem(SWEEPS, 2, M // 2, 8, K),
            vmem(SWEEPS, 2, 2, 8, K),
            vmem(SWEEPS, 2, M, K),
            vmem(SWEEPS, 2, 2, M, K),
            vmem(M, 8, K),
            vmem(2, M, 8, K),
            vmem(M, 8, K),
            vmem(M + 2, 8, K),
            vmem(2, M + 2, 8, K),
            vmem(4, M, K),
            pltpu.SemaphoreType.DMA((2, 4)),
            pltpu.SemaphoreType.DMA((M,)),
            pltpu.SemaphoreType.DMA((SWEEPS + 1, len(ROUTES))),
            pltpu.SemaphoreType.DMA((SWEEPS + 1, len(ROUTES))),
        ],
        compiler_params=pltpu.CompilerParams(collective_id=0, has_side_effects=True),
    )(field, source)


def solution(mesh):
    spec = P("gx", "gy", "gz")
    return jax.shard_map(on_device, mesh=mesh, in_specs=(spec, spec), out_specs=spec, check_vma=False)
```

profile of v0, /device:TPU:1, one launch (start us, length us, event | category | flops | bytes accessed | tf_op | source)
XLA Modules:
  0.0 39.6 jit_solution(4046537724525817579)
XLA Ops:
  0.0 36.4 %shard_map.28 = f32[16,256,128]{2,1,0:T(8,128)} custom-call(f32[16,256,128]{2,1,0:T(8,128)} %field.1, f32[16,256,128]{2,1,0:T(8,128)} %source.1), custom_call_target="tpu_custom_call" | custom-call | tf_op jit(solution)/shard_map/pallas_call | solution.py:311
  36.5 3.1 %copy.4 = f32[16,256,128]{2,1,0:T(8,128)} copy(f32[16,256,128]{2,1,0:T(8,128)} %shard_map.28) | data formatting | bytes 4194304
where the time goes:
time: 39.7 us; the launch traced here: 39.6 us
  Pallas kernels  36.4 us (92%)
  local copies, waits for them, and re-layouts  3.11 us (8%)
    pallas_call x1, Pallas kernels, on_device(): pl.pallas_call(kernel, out_shape=jax.ShapeDtypeStruct(field.shape, f32),...  36.4 us
    unnamed x1, local copies, waits for them, and re-layouts  3.11 us

commit v1 on v0

--- a/solution.py
+++ b/solution.py
@@ -29,8 +29,8 @@
     return 0 if step < 0 else 1
 
 
-def kernel(field, source, out, fbuf, sbuf, obuf, S, X, own, zout, zin, xzin, yzout, yzin,
-           sown, szin, SC, C, U, Y, isem, osem, ssem, rsem):
+def kernel(field, source, obuf, fbuf, sbuf, S, X, own, zout, zin, xzin, yzout, yzin,
+           sown, szin, sxout, sxin, SC, C, U, Y, isem, ssem, rsem):
     M = X.shape[1] - 2
     N = X.shape[2] - 2 * PAD
     T = N // 8
@@ -76,8 +76,7 @@
     def source_refs(route):
         x, y, z = route
         if x:
-            src_plane, dst_plane = ((1, M + 1), (M, 0))[side(x)]
-            return S.at[0, src_plane, rows], S.at[0, dst_plane, rows]
+            return sxout.at[side(x)], sxin.at[side(-x)]
         if y:
             src_rows, dst_rows = edge_rows[side(y)]
             return S.at[0, inner, src_rows], S.at[0, inner, dst_rows]
@@ -91,6 +90,13 @@
             device_id=target(route), device_id_type=MESH)
 
     faces = [r for r in ROUTES if sum(map(abs, r)) == 1]
+    edges = [r for r in ROUTES if sum(map(abs, r)) == 2]
+    edges.sort(key=lambda r: abs(r[0]))
+    x_faces = [r for r in faces if r[0]]
+    yz_faces = [r for a in (2, 1) for r in faces if r[a]]
+    yz_edges = [r for r in edges if not r[0]]
+    early = [r for r in edges if r[0]] + yz_faces
+    ordered = edges + yz_faces + x_faces
 
     def start(r, routes):
         for route in routes:
@@ -123,6 +129,7 @@
     outer = (lane == 0) | (lane == LANES - 1)
     odd_rows = (iota((8 * CHUNK, LANES), 0) + iota((8 * CHUNK, LANES), 1)) % 2 == 1
     outer_rows = (iota((8 * CHUNK, LANES), 1) == 0) | (iota((8 * CHUNK, LANES), 1) == LANES - 1)
+    row_of = iota((8 * CHUNK, LANES), 0)
     gap = jnp.abs(iota((LANES, LANES), 0) - iota((LANES, LANES), 1))
     beside_lanes = jnp.where(gap == 1, 1.0, 0.0).astype(bf16)
     beside_lanes = jnp.concatenate([beside_lanes, beside_lanes], 0)
@@ -166,8 +173,6 @@
             yzout[r, 1, m:m + 1] = own[r, m, 7:8]
 
     order = [0, M - 1] + list(range(1, M - 1))
-    x_routes = [r for r in ROUTES if r[0]]
-    other_routes = [r for r in ROUTES if not r[0]]
     whole_odd = (iota((N, LANES), 0) + iota((N, LANES), 1)) % 2 == 1
 
     for load in loads[:4]:
@@ -181,7 +186,7 @@
         own[0, m] = acc
     finish_pack(0)
     pl.semaphore_wait(barrier, count)
-    start(0, ROUTES)
+    start(0, ordered)
 
     for load in loads[4:]:
         load.wait()
@@ -194,7 +199,14 @@
         for t in (range(T)):
             acc = pack(acc, t, value[8 * t:8 * t + 8])
         sown[m] = acc
-    start(SWEEPS, faces)
+        if m in (0, M - 1):
+            top, bottom = value[:N // 2], pltpu.roll(value[N // 2:], 1, 1)
+            odd_half = whole_odd[:N // 2]
+            if m == 0:
+                sxout[0] = jnp.where(odd_half, bottom, top)
+            if m == M - 1:
+                sxout[1] = jnp.where(odd_half, top, bottom)
+    start(SWEEPS, yz_faces + x_faces)
 
     def update(h, m, start_row, length, wings, near=None):
         here = pl.ds(start_row, length)
@@ -208,7 +220,9 @@
             near = X[h, near + 1, here]
         total = (S[h % 2, m + 1, here] + centre) + (near + lane_sum(centre))
         total = total + (X[h, m + 1, pl.ds(start_row - 1, length)] + X[h, m + 1, pl.ds(start_row + 1, length)])
-        return (total + jnp.where(outer_rows[:length], wings, 0.0)) * f32(SIXTH)
+        if wings is not None:
+            total = total + jnp.where(outer_rows[:length], wings, 0.0)
+        return total * f32(SIXTH)
 
     def wings_of(edge, tiles):
         return jnp.concatenate([turn(edge, LANES - 2 - 4 * t) for t in tiles], 0)
@@ -217,9 +231,9 @@
 
     for r in range(SWEEPS):
         h = 2 * r
-        wait(r, ROUTES)
+        wait(r, early)
         if r == 0:
-            wait(SWEEPS, faces)
+            wait(SWEEPS, yz_faces)
             for m in range(M):
                 SC[m] = jnp.where(place == 1, szin[0, m], szin[1, m])
         for m in range(M):
@@ -231,15 +245,6 @@
         C[M + 1] = jnp.where(place == 1, xzin[r, 1, 0], xzin[r, 1, 1])
         for m in range(M + 2):
             U[0, m] = swapped(C[m])
-        small = (M, LANES)
-        spot = iota(small, 1) % 4
-        ends = (iota(small, 1) == 0) | (iota(small, 1) == LANES - 1)
-        low_corner = jnp.where(spot == 1, yzin[r, 0, 0], yzin[r, 0, 1])
-        high_corner = jnp.where(spot == 1, yzin[r, 1, 0], yzin[r, 1, 1])
-        Y[0] = turn(low_corner, -4 * (T - 1))
-        Y[1] = turn(high_corner, 4 * (T - 1))
-        Y[2] = jnp.where(ends, turn(swapped(low_corner), LANES - 2 - 4 * (T - 1)), 0.0)
-        Y[3] = jnp.where(ends, turn(swapped(high_corner), LANES - 2), 0.0)
         for m in range(M):
             a, b = zin[r, 0, m % H], zin[r, 1, m % H]
             if m >= H:
@@ -249,34 +254,55 @@
             across = turn(jnp.where(place == 0, a, mine), 1) + turn(jnp.where(place == 3, b, mine), -1)
             above = turn(centre, -1, 0)
             above = jnp.where(sub == 7, turn(above, -4), above)
-            above = jnp.where((sub == 7) & (group == T - 1), Y[1, m:m + 1], above)
+            above = jnp.where((sub == 7) & (group == T - 1), 0.0, above)
             below = turn(centre, 1, 0)
             below = jnp.where(sub == 0, turn(below, 4), below)
-            below = jnp.where((sub == 0) & (group == 0), Y[0, m:m + 1], below)
+            below = jnp.where((sub == 0) & (group == 0), 0.0, below)
             near = jnp.where(odd8, C[m + 2], C[m])
             red = (SC[m] + centre + near + (across + (above + below))) * f32(SIXTH)
             U[1, m] = swapped(red)
-        for m in range(M):
+        def red_plane(m, near=None):
             for tiles in chunks:
                 begin = PAD + 8 * tiles[0]
-                value = update(h, m, begin, 8 * len(tiles), wings_of(U[0, m + 1], tiles))
-                X[h + 1, m + 1, pl.ds(begin, 8 * len(tiles))] = value
-            for k, begin in enumerate((PAD - 8, PAD + N)):
-                X[h + 1, m + 1, pl.ds(begin, 8)] = update(
-                    h, m, begin, 8, jnp.broadcast_to(Y[2 + k, m:m + 1], (8, LANES)))
+                X[h + 1, m + 1, pl.ds(begin, 8 * len(tiles))] = update(
+                    h, m, begin, 8 * len(tiles), wings_of(U[0, m + 1], tiles), near)
+
+        for m in range(1, M - 1):
+            red_plane(m)
+        for m in range(M):
+            for begin in (PAD - 8, PAD + N):
+                X[h + 1, m + 1, pl.ds(begin, 8)] = update(h, m, begin, 8, None)
+        wait(r, x_faces)
+        if r == 0:
+            wait(SWEEPS, x_faces)
+            for k, plane in enumerate((0, M + 1)):
+                @pl.when(has[k])
+                def _(k=k, plane=plane):
+                    half = sxin[k]
+                    S[0, plane, pl.ds(PAD, N // 2)] = half
+                    S[0, plane, pl.ds(PAD + N // 2, N // 2)] = pltpu.roll(half, LANES - 1, 1)
         for k, (m, near) in enumerate(((-1, 0), (M, M - 1))):
-            @pl.when(has[k])
-            def _(m=m, near=near):
-                for tiles in chunks:
-                    begin = PAD + 8 * tiles[0]
-                    X[h + 1, m + 1, pl.ds(begin, 8 * len(tiles))] = update(
-                        h, m, begin, 8 * len(tiles), wings_of(U[0, m + 1], tiles), near)
+            pl.when(has[k])(functools.partial(red_plane, m, near))
+        red_plane(0)
+        red_plane(M - 1)
+        wait(r, yz_edges)
+        small = (M, LANES)
+        spot = iota(small, 1) % 4
+        ends = (iota(small, 1) == 0) | (iota(small, 1) == LANES - 1)
+        low_corner = jnp.where(spot == 1, yzin[r, 0, 0], yzin[r, 0, 1])
+        high_corner = jnp.where(spot == 1, yzin[r, 1, 0], yzin[r, 1, 1])
+        Y[0] = jnp.where(ends, turn(swapped(low_corner), LANES - 2 - 4 * (T - 1)), 0.0) * f32(1.0 / 18.0)
+        Y[1] = jnp.where(ends, turn(swapped(high_corner), LANES - 2), 0.0) * f32(1.0 / 18.0)
         h += 1
         for number, m in enumerate(order):
             acc = jnp.zeros((8, LANES), f32)
             for tiles in chunks:
                 begin, length = PAD + 8 * tiles[0], 8 * len(tiles)
                 value = update(h, m, begin, length, wings_of(U[1, m], tiles))
+                if tiles[0] == 0:
+                    value = value + jnp.where(row_of[:length] == 0, Y[0, m:m + 1], 0.0)
+                if tiles[-1] == T - 1:
+                    value = value + jnp.where(row_of[:length] == length - 1, Y[1, m:m + 1], 0.0)
                 if r < SWEEPS - 1:
                     X[h + 1, m + 1, pl.ds(begin, length)] = value
                     for t in tiles:
@@ -287,21 +313,15 @@
                     obuf[2 * m + 1, pl.ds(begin - PAD, length)] = jnp.where(odd_rows[:length], red, value)
             if r < SWEEPS - 1:
                 own[r + 1, m] = acc
-                if number == 1:
-                    start(r + 1, x_routes)
-            else:
-                pltpu.make_async_copy(obuf.at[pl.ds(2 * m, 2)], out.at[pl.ds(2 * m, 2)], osem.at[m]).start()
         if r < SWEEPS - 1:
             finish_pack(r + 1)
-            start(r + 1, other_routes)
+            start(r + 1, ordered)
 
     for r in range(SWEEPS):
         for route in ROUTES:
             guarded(route[0], lambda route=route: remote(r, route).wait_send())
     for route in faces:
         guarded(route[0], lambda route=route: remote(SWEEPS, route).wait_send())
-    for m in range(M):
-        pltpu.make_async_copy(obuf.at[pl.ds(2 * m, 2)], out.at[pl.ds(2 * m, 2)], osem.at[m]).wait()
 
 
 def on_device(field, source):
@@ -311,10 +331,10 @@
     return pl.pallas_call(
         kernel,
         out_shape=jax.ShapeDtypeStruct(field.shape, f32),
-        in_specs=[pl.BlockSpec(memory_space=pl.ANY)] * 2,
-        out_specs=pl.BlockSpec(memory_space=pl.ANY),
+        in_specs=[pl.BlockSpec(memory_space=pltpu.HBM)] * 2,
+        out_specs=pl.BlockSpec(memory_space=pltpu.VMEM),
         scratch_shapes=[
-            vmem(L, N, K), vmem(L, N, K), vmem(L, N, K),
+            vmem(L, N, K), vmem(L, N, K),
             vmem(2, M + 2, N + 2 * PAD, K),
             vmem(HALF, M + 2, N + 2 * PAD, K),
             vmem(SWEEPS, M, 8, K),
@@ -325,17 +345,17 @@
             vmem(SWEEPS, 2, 2, M, K),
             vmem(M, 8, K),
             vmem(2, M, 8, K),
+            vmem(2, N // 2, K), vmem(2, N // 2, K),
             vmem(M, 8, K),
             vmem(M + 2, 8, K),
             vmem(2, M + 2, 8, K),
-            vmem(4, M, K),
+            vmem(2, M, K),
             pltpu.SemaphoreType.DMA((2, 4)),
-            pltpu.SemaphoreType.DMA((M,)),
             pltpu.SemaphoreType.DMA((SWEEPS + 1, len(ROUTES))),
             pltpu.SemaphoreType.DMA((SWEEPS + 1, len(ROUTES))),
         ],
-        compiler_params=pltpu.CompilerParams(collective_id=0, has_side_effects=True),
-    )(field, source)
+        compiler_params=pltpu.CompilerParams(collective_id=0, has_side_effects=True, vmem_limit_bytes=40 << 20),
+    )(pltpu.with_memory_space_constraint(field, pltpu.HBM), pltpu.with_memory_space_constraint(source, pltpu.HBM))
 
 
 def solution(mesh):

time: 39.7 us -> 34.4 us (0.87)
  Pallas kernels: 36.4 us -> 33 us
  local copies, waits for them, and re-layouts: 3.11 us -> 1.32 us
    pallas_call x1, Pallas kernels: 36.4 us -> 33 us  [on_device(): pl.pallas_call(kernel, out_shape=jax.ShapeDtypeStruct(field.shape, f32),...]
    unnamed x1, local copies, waits for them, and re-layouts: 3.11 us -> 1.32 us
where the time goes in v1:
time: 34.4 us; the launch traced here: 34.3 us
  Pallas kernels  33 us (96%)
  local copies, waits for them, and re-layouts  1.32 us (4%)
    pallas_call x1, Pallas kernels, on_device(): pl.pallas_call(kernel, out_shape=jax.ShapeDtypeStruct(field.shape, f32),...  33 us
    unnamed x1, local copies, waits for them, and re-layouts  1.32 us

profile of v1, /device:TPU:1, one launch (start us, length us, event | category | flops | bytes accessed | tf_op | source)
XLA Modules:
  0.0 34.3 jit_solution(15640828214942948184)
XLA Ops:
  0.0 33.0 %shard_map.28 = f32[16,256,128]{2,1,0:T(8,128)S(1)} custom-call(f32[16,256,128]{2,1,0:T(8,128)} %field.1, f32[16,256,128]{2,1,0:T(8,128)} %source.1), custom_call_target="tpu_custom_call" | custom-call | tf_op jit(solution)/shard_map/pallas_call | solution.py:331
  33.0 1.3 %copy.4 = f32[16,256,128]{2,1,0:T(8,128)} copy(f32[16,256,128]{2,1,0:T(8,128)S(1)} %shard_map.28) | data formatting | bytes 4194304

commit v2 on v1

--- a/solution.py
+++ b/solution.py
@@ -30,7 +30,7 @@
 
 
 def kernel(field, source, obuf, fbuf, sbuf, S, X, own, zout, zin, xzin, yzout, yzin,
-           sown, szin, sxout, sxin, SC, C, U, Y, isem, ssem, rsem):
+           sown, szin, sxout, sxin, SC, C, U, Y, SZ, V, DZ, PK, DY, DYR, DR, DX, isem, ssem, rsem):
     M = X.shape[1] - 2
     N = X.shape[2] - 2 * PAD
     T = N // 8
@@ -130,6 +130,7 @@
     odd_rows = (iota((8 * CHUNK, LANES), 0) + iota((8 * CHUNK, LANES), 1)) % 2 == 1
     outer_rows = (iota((8 * CHUNK, LANES), 1) == 0) | (iota((8 * CHUNK, LANES), 1) == LANES - 1)
     row_of = iota((8 * CHUNK, LANES), 0)
+    rim_rows = (iota((8 * CHUNK, LANES), 1) < 2) | (iota((8 * CHUNK, LANES), 1) >= LANES - 2)
     gap = jnp.abs(iota((LANES, LANES), 0) - iota((LANES, LANES), 1))
     beside_lanes = jnp.where(gap == 1, 1.0, 0.0).astype(bf16)
     beside_lanes = jnp.concatenate([beside_lanes, beside_lanes], 0)
@@ -172,6 +173,11 @@
             yzout[r, 0, m:m + 1] = own[r, m, 0:1]
             yzout[r, 1, m:m + 1] = own[r, m, 7:8]
 
+    V[0] = jnp.zeros((8, LANES), f32)
+    V[M + 1] = jnp.zeros((8, LANES), f32)
+    for k in range(2):
+        DR[k, 0:8] = jnp.zeros((8, LANES), f32)
+        DR[k, N + 8:N + 16] = jnp.zeros((8, LANES), f32)
     order = [0, M - 1] + list(range(1, M - 1))
     whole_odd = (iota((N, LANES), 0) + iota((N, LANES), 1)) % 2 == 1
 
@@ -212,25 +218,83 @@
         here = pl.ds(start_row, length)
         centre = X[h, m + 1, here]
         if near is None:
-            low, high = X[h, m, here], X[h, m + 2, here]
-            if h % 2:
-                low, high = high, low
-            near = jnp.where(odd_rows[:length], high, low)
+            near = jnp.where(odd_rows[:length], X[h, m + 2, here], X[h, m, here])
         else:
             near = X[h, near + 1, here]
-        total = (S[h % 2, m + 1, here] + centre) + (near + lane_sum(centre))
+        total = (S[0, m + 1, here] + centre) + (near + lane_sum(centre))
         total = total + (X[h, m + 1, pl.ds(start_row - 1, length)] + X[h, m + 1, pl.ds(start_row + 1, length)])
         if wings is not None:
             total = total + jnp.where(outer_rows[:length], wings, 0.0)
         return total * f32(SIXTH)
 
+    def inside(h, m, tiles):
+        start_row, length = PAD + 8 * tiles[0], 8 * len(tiles)
+        here = pl.ds(start_row, length)
+        centre = X[h, m + 1, here]
+        low = X[h, m, here] if m > 0 else 0.0
+        high = X[h, m + 2, here] if m < M - 1 else 0.0
+        if h % 2:
+            low, high = high, low
+        total = (S[h % 2, m + 1, here] + centre) + (jnp.where(odd_rows[:length], high, low) + lane_sum(centre))
+        if tiles[0] == 0:
+            down = jnp.where(row_of[:length] == 0, 0.0, pltpu.roll(centre, 1, 0))
+        else:
+            down = X[h, m + 1, pl.ds(start_row - 1, length)]
+        if tiles[-1] == T - 1:
+            above = jnp.where(row_of[:length] == length - 1, 0.0, pltpu.roll(centre, length - 1, 0))
+        else:
+            above = X[h, m + 1, pl.ds(start_row + 1, length)]
+        return (total + (down + above)) * f32(SIXTH)
+
     def wings_of(edge, tiles):
         return jnp.concatenate([turn(edge, LANES - 2 - 4 * t) for t in tiles], 0)
 
+    def spread(edge, tiles):
+        return jnp.where(rim_rows[:8 * len(tiles)], wings_of(edge, tiles), 0.0)
+
+    def shifted(value):
+        above = turn(value, -1, 0)
+        above = jnp.where(sub == 7, turn(above, -4), above)
+        above = jnp.where((sub == 7) & (group == T - 1), 0.0, above)
+        below = turn(value, 1, 0)
+        below = jnp.where(sub == 0, turn(below, 4), below)
+        below = jnp.where((sub == 0) & (group == 0), 0.0, below)
+        return above + below
+
     chunks = [range(c, min(c + CHUNK, T)) for c in range(0, T, CHUNK)]
+    middle = (place == 1) | (place == 2)
+    zero8 = jnp.zeros((8, LANES), f32)
+
+    def padded(tiles, low, high):
+        parts = [zero8] * len(tiles)
+        if tiles[0] == 0:
+            parts[0] = low
+        if tiles[-1] == T - 1:
+            parts[-1] = high
+        return jnp.concatenate(parts, 0) if tiles[0] == 0 or tiles[-1] == T - 1 else None
 
     for r in range(SWEEPS):
         h = 2 * r
+        ended = r == SWEEPS - 1
+        if r > 0:
+            for m in range(1, M - 1):
+                for tiles in chunks:
+                    tiles = [t for t in tiles if 0 < t < T - 1]
+                    here = pl.ds(PAD + 8 * tiles[0], 8 * len(tiles))
+                    X[h, m + 1, here] = X[h, m + 1, here] + spread(DZ[m], tiles)
+        for m in range(M):
+            for tiles in chunks:
+                X[h + 1, m + 1, pl.ds(PAD + 8 * tiles[0], 8 * len(tiles))] = inside(h, m, tiles)
+        for m in range(M):
+            acc = zero8
+            for tiles in chunks:
+                value = inside(h + 1, m, tiles)
+                X[h + 2, m + 1, pl.ds(PAD + 8 * tiles[0], 8 * len(tiles))] = value
+                if not ended and 0 < m < M - 1:
+                    for t in tiles:
+                        acc = pack(acc, t, value[8 * (t - tiles[0]):8 * (t - tiles[0]) + 8])
+            PK[m] = acc
+
         wait(r, early)
         if r == 0:
             wait(SWEEPS, yz_faces)
@@ -240,51 +304,59 @@
             a, b = zin[r, 0, m % H], zin[r, 1, m % H]
             if m >= H:
                 a, b = turn(a, -2), turn(b, 2)
+            mine = own[r, m]
             C[m + 1] = jnp.where(place == 1, a, b)
+            SZ[m] = turn(jnp.where(place == 0, a, mine), 1) + turn(jnp.where(place == 3, b, mine), -1)
         C[0] = jnp.where(place == 1, xzin[r, 0, 0], xzin[r, 0, 1])
         C[M + 1] = jnp.where(place == 1, xzin[r, 1, 0], xzin[r, 1, 1])
-        for m in range(M + 2):
-            U[0, m] = swapped(C[m])
-        for m in range(M):
-            a, b = zin[r, 0, m % H], zin[r, 1, m % H]
-            if m >= H:
-                a, b = turn(a, -2), turn(b, 2)
-            mine = own[r, m]
+        U[0] = swapped(C[0])
+        U[1] = swapped(C[M + 1])
+        for m in range(M):
+            V[m + 1] = jnp.where(middle, swapped(C[m + 1]), 0.0) * f32(SIXTH)
+        for m in range(M):
             centre = C[m + 1]
-            across = turn(jnp.where(place == 0, a, mine), 1) + turn(jnp.where(place == 3, b, mine), -1)
-            above = turn(centre, -1, 0)
-            above = jnp.where(sub == 7, turn(above, -4), above)
-            above = jnp.where((sub == 7) & (group == T - 1), 0.0, above)
-            below = turn(centre, 1, 0)
-            below = jnp.where(sub == 0, turn(below, 4), below)
-            below = jnp.where((sub == 0) & (group == 0), 0.0, below)
             near = jnp.where(odd8, C[m + 2], C[m])
-            red = (SC[m] + centre + near + (across + (above + below))) * f32(SIXTH)
-            U[1, m] = swapped(red)
-        def red_plane(m, near=None):
-            for tiles in chunks:
-                begin = PAD + 8 * tiles[0]
-                X[h + 1, m + 1, pl.ds(begin, 8 * len(tiles))] = update(
-                    h, m, begin, 8 * len(tiles), wings_of(U[0, m + 1], tiles), near)
-
-        for m in range(1, M - 1):
-            red_plane(m)
-        for m in range(M):
-            for begin in (PAD - 8, PAD + N):
+            red = (SC[m] + centre + near + (SZ[m] + shifted(centre))) * f32(SIXTH)
+            mine = V[m + 1]
+            near = jnp.where(odd8, V[m], V[m + 2])
+            total = (swapped(red) + mine) + (near + shifted(mine))
+            DZ[m] = jnp.where(middle, total, jnp.where(place == 0, turn(mine, -1), turn(mine, 1))) * f32(SIXTH)
+        for k, (begin, row, end, following) in enumerate(((PAD - 8, PAD - 1, 0, 1), (PAD + N, PAD + N, 7, 6))):
+            for m in range(M):
                 X[h + 1, m + 1, pl.ds(begin, 8)] = update(h, m, begin, 8, None)
+            change = [jnp.broadcast_to(X[h, m + 1, row:row + 1], (8, LANES)) * f32(SIXTH) for m in range(M)]
+            sums = lane_sum(jnp.concatenate(change, 0))
+            for m in range(M):
+                low = change[m - 1] if m > 0 else 0.0
+                high = change[m + 1] if m < M - 1 else 0.0
+                near = jnp.where(lane % 2 == 1 - k, low, high)
+                total = (X[h + 1, m + 1, row:row + 1] + change[m]) + (near + sums[8 * m:8 * m + 8])
+                DY[k, m] = jnp.where(sub == end, total, jnp.where(sub == following, change[m], 0.0)) * f32(SIXTH)
+                if ended:
+                    DYR[k, m] = jnp.where(sub == end, change[m], 0.0)
         wait(r, x_faces)
         if r == 0:
             wait(SWEEPS, x_faces)
             for k, plane in enumerate((0, M + 1)):
-                @pl.when(has[k])
-                def _(k=k, plane=plane):
-                    half = sxin[k]
-                    S[0, plane, pl.ds(PAD, N // 2)] = half
-                    S[0, plane, pl.ds(PAD + N // 2, N // 2)] = pltpu.roll(half, LANES - 1, 1)
+                half = sxin[k]
+                S[0, plane, pl.ds(PAD, N // 2)] = half
+                S[0, plane, pl.ds(PAD + N // 2, N // 2)] = pltpu.roll(half, LANES - 1, 1)
         for k, (m, near) in enumerate(((-1, 0), (M, M - 1))):
-            pl.when(has[k])(functools.partial(red_plane, m, near))
-        red_plane(0)
-        red_plane(M - 1)
+            for tiles in chunks:
+                begin, length = PAD + 8 * tiles[0], 8 * len(tiles)
+                odd = odd_rows[:length]
+                red = update(h, m, begin, length, wings_of(U[k], tiles), near)
+                bare = X[h, m + 1, pl.ds(begin, length)] * f32(SIXTH)
+                if k == 0:
+                    red, bare = jnp.where(odd, red, 0.0), jnp.where(odd, 0.0, bare)
+                else:
+                    red, bare = jnp.where(odd, 0.0, red), jnp.where(odd, bare, 0.0)
+                DR[k, pl.ds(8 + 8 * tiles[0], length)] = bare
+                DX[k, pl.ds(8 * tiles[0], length)] = jnp.where(has[k], red, 0.0) + (bare + lane_sum(bare))
+            for tiles in chunks:
+                begin, length = 8 * tiles[0], 8 * len(tiles)
+                here = pl.ds(begin, length)
+                DX[k, here] = (DX[k, here] + (DR[k, pl.ds(7 + begin, length)] + DR[k, pl.ds(9 + begin, length)])) * f32(SIXTH)
         wait(r, yz_edges)
         small = (M, LANES)
         spot = iota(small, 1) % 4
@@ -293,29 +365,50 @@
         high_corner = jnp.where(spot == 1, yzin[r, 1, 0], yzin[r, 1, 1])
         Y[0] = jnp.where(ends, turn(swapped(low_corner), LANES - 2 - 4 * (T - 1)), 0.0) * f32(1.0 / 18.0)
         Y[1] = jnp.where(ends, turn(swapped(high_corner), LANES - 2), 0.0) * f32(1.0 / 18.0)
-        h += 1
-        for number, m in enumerate(order):
-            acc = jnp.zeros((8, LANES), f32)
-            for tiles in chunks:
-                begin, length = PAD + 8 * tiles[0], 8 * len(tiles)
-                value = update(h, m, begin, length, wings_of(U[1, m], tiles))
-                if tiles[0] == 0:
-                    value = value + jnp.where(row_of[:length] == 0, Y[0, m:m + 1], 0.0)
-                if tiles[-1] == T - 1:
-                    value = value + jnp.where(row_of[:length] == length - 1, Y[1, m:m + 1], 0.0)
-                if r < SWEEPS - 1:
-                    X[h + 1, m + 1, pl.ds(begin, length)] = value
+        for m in range(M):
+            DY[0, m] = DY[0, m] + jnp.where(sub == 0, Y[0, m:m + 1], 0.0)
+            DY[1, m] = DY[1, m] + jnp.where(sub == 7, Y[1, m:m + 1], 0.0)
+
+        def black(m, tiles):
+            value = X[h + 2, m + 1, pl.ds(PAD + 8 * tiles[0], 8 * len(tiles))] + spread(DZ[m], tiles)
+            extra = padded(tiles, DY[0, m], DY[1, m])
+            if extra is not None:
+                value = value + extra
+            if m in (0, M - 1):
+                value = value + DX[0 if m == 0 else 1, pl.ds(8 * tiles[0], 8 * len(tiles))]
+            return value
+
+        if not ended:
+            for m in (0, M - 1):
+                acc = zero8
+                for tiles in chunks:
+                    value = black(m, tiles)
+                    X[h + 2, m + 1, pl.ds(PAD + 8 * tiles[0], 8 * len(tiles))] = value
                     for t in tiles:
                         acc = pack(acc, t, value[8 * (t - tiles[0]):8 * (t - tiles[0]) + 8])
-                else:
-                    red = X[h, m + 1, pl.ds(begin, length)]
-                    obuf[2 * m, pl.ds(begin - PAD, length)] = jnp.where(odd_rows[:length], value, red)
-                    obuf[2 * m + 1, pl.ds(begin - PAD, length)] = jnp.where(odd_rows[:length], red, value)
-            if r < SWEEPS - 1:
                 own[r + 1, m] = acc
-        if r < SWEEPS - 1:
+            start(r + 1, [q for q in edges if q[0]] + x_faces)
+            for m in range(1, M - 1):
+                for t in (0, T - 1):
+                    X[h + 2, m + 1, pl.ds(PAD + 8 * t, 8)] = black(m, [t])
+                low = jnp.where(group == 0, turn(DY[0, m], 2), 0.0)
+                high = jnp.where(group == T - 1, turn(DY[1, m], 4 * T - 2), 0.0)
+                own[r + 1, m] = (PK[m] + DZ[m]) + (low + high)
             finish_pack(r + 1)
-            start(r + 1, ordered)
+            start(r + 1, [q for q in ordered if not q[0]])
+        else:
+            for m in range(M):
+                for tiles in chunks:
+                    begin, length = 8 * tiles[0], 8 * len(tiles)
+                    value = black(m, tiles)
+                    red = X[h + 1, m + 1, pl.ds(PAD + begin, length)] + spread(V[m + 1], tiles)
+                    extra = padded(tiles, DYR[0, m], DYR[1, m])
+                    if extra is not None:
+                        red = red + extra
+                    if m in (0, M - 1):
+                        red = red + DR[0 if m == 0 else 1, pl.ds(8 + begin, length)]
+                    obuf[2 * m, pl.ds(begin, length)] = jnp.where(odd_rows[:length], value, red)
+                    obuf[2 * m + 1, pl.ds(begin, length)] = jnp.where(odd_rows[:length], red, value)
 
     for r in range(SWEEPS):
         for route in ROUTES:
@@ -336,7 +429,7 @@
         scratch_shapes=[
             vmem(L, N, K), vmem(L, N, K),
             vmem(2, M + 2, N + 2 * PAD, K),
-            vmem(HALF, M + 2, N + 2 * PAD, K),
+            vmem(HALF + 1, M + 2, N + 2 * PAD, K),
             vmem(SWEEPS, M, 8, K),
             vmem(SWEEPS, 2, M // 2, 8, K),
             vmem(SWEEPS, 2, M // 2, 8, K),
@@ -348,8 +441,16 @@
             vmem(2, N // 2, K), vmem(2, N // 2, K),
             vmem(M, 8, K),
             vmem(M + 2, 8, K),
-            vmem(2, M + 2, 8, K),
+            vmem(2, 8, K),
             vmem(2, M, K),
+            vmem(M, 8, K),
+            vmem(M + 2, 8, K),
+            vmem(M, 8, K),
+            vmem(M, 8, K),
+            vmem(2, M, 8, K),
+            vmem(2, M, 8, K),
+            vmem(2, N + 16, K),
+            vmem(2, N, K),
             pltpu.SemaphoreType.DMA((2, 4)),
             pltpu.SemaphoreType.DMA((SWEEPS + 1, len(ROUTES))),
             pltpu.SemaphoreType.DMA((SWEEPS + 1, len(ROUTES))),

time: 34.4 us -> 31.7 us (0.922)
  Pallas kernels: 33 us -> 30.3 us
    pallas_call x1, Pallas kernels: 33 us -> 30.3 us  [on_device(): pl.pallas_call(kernel, out_shape=jax.ShapeDtypeStruct(field.shape, f32),...]
where the time goes in v2:
time: 31.7 us; the launch traced here: 31.6 us
  Pallas kernels  30.3 us (96%)
  local copies, waits for them, and re-layouts  1.32 us (4%)
    pallas_call x1, Pallas kernels, on_device(): pl.pallas_call(kernel, out_shape=jax.ShapeDtypeStruct(field.shape, f32),...  30.3 us
    unnamed x1, local copies, waits for them, and re-layouts  1.32 us

profile of v2, /device:TPU:1, one launch (start us, length us, event | category | flops | bytes accessed | tf_op | source)
XLA Modules:
  0.0 31.6 jit_solution(14150663394661846868)
XLA Ops:
  0.0 30.3 %shard_map.28 = f32[16,256,128]{2,1,0:T(8,128)S(1)} custom-call(f32[16,256,128]{2,1,0:T(8,128)} %field.1, f32[16,256,128]{2,1,0:T(8,128)} %source.1), custom_call_target="tpu_custom_call" | custom-call | tf_op jit(solution)/shard_map/pallas_call | solution.py:424
  30.3 1.3 %copy.4 = f32[16,256,128]{2,1,0:T(8,128)} copy(f32[16,256,128]{2,1,0:T(8,128)S(1)} %shard_map.28) | data formatting | bytes 4194304

commit v3 on v2

--- a/solution.py
+++ b/solution.py
@@ -30,7 +30,7 @@
 
 
 def kernel(field, source, obuf, fbuf, sbuf, S, X, own, zout, zin, xzin, yzout, yzin,
-           sown, szin, sxout, sxin, SC, C, U, Y, SZ, V, DZ, PK, DY, DYR, DR, DX, isem, ssem, rsem):
+           sown, szout, szin, sxout, sxin, SC, C, U, Y, SZ, V, DZ, PK, DY, DYR, DR, DX, isem, ssem, rsem):
     M = X.shape[1] - 2
     N = X.shape[2] - 2 * PAD
     T = N // 8
@@ -80,7 +80,7 @@
         if y:
             src_rows, dst_rows = edge_rows[side(y)]
             return S.at[0, inner, src_rows], S.at[0, inner, dst_rows]
-        return sown, szin.at[side(-z)]
+        return szout.at[side(z)], szin.at[side(-z)]
 
     def remote(r, route):
         pair = refs(r, route) if r < SWEEPS else source_refs(route)
@@ -96,7 +96,7 @@
     yz_faces = [r for a in (2, 1) for r in faces if r[a]]
     yz_edges = [r for r in edges if not r[0]]
     early = [r for r in edges if r[0]] + yz_faces
-    ordered = edges + yz_faces + x_faces
+    ordered = yz_edges + [q for q in faces if q[2]] + [q for q in edges if q[0]] + x_faces + [q for q in faces if q[1]]
 
     def start(r, routes):
         for route in routes:
@@ -107,11 +107,13 @@
             guarded(-route[0], lambda route=route: remote(r, route).wait_recv())
 
     planes = 2 * M // 4
-    loads = []
-    for slot, (big, small) in enumerate(((field, fbuf), (source, sbuf))):
-        for part in (0, 3, 1, 2):
-            here = pl.ds(part * planes, planes)
-            loads.append(pltpu.make_async_copy(big.at[here], small.at[here], isem.at[slot, part]))
+    spans = [(source, sbuf, 0, 2), (source, sbuf, 2 * M - 2, 2)]
+    spans += [(field, fbuf, part * planes, planes) for part in range(4)]
+    spans += [(source, sbuf, 2, 2 * M - 4)] if M > 2 else []
+    loads = [
+        pltpu.make_async_copy(big.at[pl.ds(first_plane, n)], small.at[pl.ds(first_plane, n)], isem.at[number])
+        for number, (big, small, first_plane, n) in enumerate(spans)
+    ]
     for load in loads:
         load.start()
     barrier = pltpu.get_barrier_semaphore()
@@ -147,6 +149,8 @@
         where = iota(value.shape, 1) % 4
         return jnp.where(where == 1, turn(value, -1), turn(value, 1))
 
+    zero8 = jnp.zeros((8, LANES), f32)
+
     def pack(acc, t, tile):
         return jnp.where(group == t, turn(tile, 4 * t + 2), acc)
 
@@ -181,7 +185,23 @@
     order = [0, M - 1] + list(range(1, M - 1))
     whole_odd = (iota((N, LANES), 0) + iota((N, LANES), 1)) % 2 == 1
 
-    for load in loads[:4]:
+    def split_source(m):
+        even_plane, odd_plane = sbuf[2 * m], sbuf[2 * m + 1]
+        value = jnp.where(whole_odd, odd_plane, even_plane)
+        S[0, m + 1, rows] = value
+        S[1, m + 1, rows] = jnp.where(whole_odd, even_plane, odd_plane)
+        return value
+
+    for load in loads[:2]:
+        load.wait()
+    for k, m in enumerate((0, M - 1)):
+        value = split_source(m)
+        top, bottom = value[:N // 2], pltpu.roll(value[N // 2:], 1, 1)
+        sxout[k] = jnp.where(whole_odd[:N // 2], (bottom, top)[k], (top, bottom)[k])
+    pl.semaphore_wait(barrier, count)
+    start(SWEEPS, x_faces)
+
+    for load in loads[2:6]:
         load.wait()
     for m in order:
         value = jnp.where(whole_odd, fbuf[2 * m], fbuf[2 * m + 1])
@@ -191,28 +211,23 @@
             acc = pack(acc, t, value[8 * t:8 * t + 8])
         own[0, m] = acc
     finish_pack(0)
-    pl.semaphore_wait(barrier, count)
     start(0, ordered)
 
-    for load in loads[4:]:
+    for load in loads[6:]:
         load.wait()
-    for m in order:
-        even_plane, odd_plane = sbuf[2 * m], sbuf[2 * m + 1]
-        value = jnp.where(whole_odd, odd_plane, even_plane)
-        S[0, m + 1, rows] = value
-        S[1, m + 1, rows] = jnp.where(whole_odd, even_plane, odd_plane)
-        acc = jnp.zeros((8, LANES), f32)
-        for t in (range(T)):
+    for m in range(M):
+        value = S[0, m + 1, rows] if m in (0, M - 1) else split_source(m)
+        acc = zero8
+        for t in range(T):
             acc = pack(acc, t, value[8 * t:8 * t + 8])
         sown[m] = acc
-        if m in (0, M - 1):
-            top, bottom = value[:N // 2], pltpu.roll(value[N // 2:], 1, 1)
-            odd_half = whole_odd[:N // 2]
-            if m == 0:
-                sxout[0] = jnp.where(odd_half, bottom, top)
-            if m == M - 1:
-                sxout[1] = jnp.where(odd_half, top, bottom)
-    start(SWEEPS, yz_faces + x_faces)
+    for q in range(-(-M // 4)):
+        ends = [zero8, zero8]
+        for i in range(min(4, M - 4 * q)):
+            for k in range(2):
+                ends[k] = jnp.where(place == i, turn(sown[4 * q + i], i - (2, 1)[k]), ends[k])
+        szout[0, q], szout[1, q] = ends
+    start(SWEEPS, yz_faces)
 
     def update(h, m, start_row, length, wings, near=None):
         here = pl.ds(start_row, length)
@@ -263,7 +278,6 @@
 
     chunks = [range(c, min(c + CHUNK, T)) for c in range(0, T, CHUNK)]
     middle = (place == 1) | (place == 2)
-    zero8 = jnp.zeros((8, LANES), f32)
 
     def padded(tiles, low, high):
         parts = [zero8] * len(tiles)
@@ -299,7 +313,8 @@
         if r == 0:
             wait(SWEEPS, yz_faces)
             for m in range(M):
-                SC[m] = jnp.where(place == 1, szin[0, m], szin[1, m])
+                q, i = divmod(m, 4)
+                SC[m] = jnp.where(place == 1, turn(szin[0, q], 1 - i), turn(szin[1, q], 2 - i))
         for m in range(M):
             a, b = zin[r, 0, m % H], zin[r, 1, m % H]
             if m >= H:
@@ -334,6 +349,31 @@
                 DY[k, m] = jnp.where(sub == end, total, jnp.where(sub == following, change[m], 0.0)) * f32(SIXTH)
                 if ended:
                     DYR[k, m] = jnp.where(sub == end, change[m], 0.0)
+        def black(m, tiles):
+            value = X[h + 2, m + 1, pl.ds(PAD + 8 * tiles[0], 8 * len(tiles))] + spread(DZ[m], tiles)
+            extra = padded(tiles, DY[0, m], DY[1, m])
+            if extra is not None:
+                value = value + extra
+            if m in (0, M - 1):
+                value = value + DX[0 if m == 0 else 1, pl.ds(8 * tiles[0], 8 * len(tiles))]
+            return value
+
+        def finished(m):
+            for tiles in chunks:
+                begin, length = 8 * tiles[0], 8 * len(tiles)
+                value = black(m, tiles)
+                red = X[h + 1, m + 1, pl.ds(PAD + begin, length)] + spread(V[m + 1], tiles)
+                extra = padded(tiles, DYR[0, m], DYR[1, m])
+                if extra is not None:
+                    red = red + extra
+                if m in (0, M - 1):
+                    red = red + DR[0 if m == 0 else 1, pl.ds(8 + begin, length)]
+                obuf[2 * m, pl.ds(begin, length)] = jnp.where(odd_rows[:length], value, red)
+                obuf[2 * m + 1, pl.ds(begin, length)] = jnp.where(odd_rows[:length], red, value)
+
+        if ended:
+            for m in range(1, M - 1):
+                finished(m)
         wait(r, x_faces)
         if r == 0:
             wait(SWEEPS, x_faces)
@@ -366,17 +406,13 @@
         Y[0] = jnp.where(ends, turn(swapped(low_corner), LANES - 2 - 4 * (T - 1)), 0.0) * f32(1.0 / 18.0)
         Y[1] = jnp.where(ends, turn(swapped(high_corner), LANES - 2), 0.0) * f32(1.0 / 18.0)
         for m in range(M):
-            DY[0, m] = DY[0, m] + jnp.where(sub == 0, Y[0, m:m + 1], 0.0)
-            DY[1, m] = DY[1, m] + jnp.where(sub == 7, Y[1, m:m + 1], 0.0)
-
-        def black(m, tiles):
-            value = X[h + 2, m + 1, pl.ds(PAD + 8 * tiles[0], 8 * len(tiles))] + spread(DZ[m], tiles)
-            extra = padded(tiles, DY[0, m], DY[1, m])
-            if extra is not None:
-                value = value + extra
-            if m in (0, M - 1):
-                value = value + DX[0 if m == 0 else 1, pl.ds(8 * tiles[0], 8 * len(tiles))]
-            return value
+            for k, (end, spot) in enumerate(((0, pl.ds(0, 8)), (7, pl.ds(N - 8, 8)))):
+                corner = jnp.where(sub == end, Y[k, m:m + 1], 0.0)
+                if ended and 0 < m < M - 1:
+                    obuf[2 * m, spot] = obuf[2 * m, spot] + jnp.where(odd8, corner, 0.0)
+                    obuf[2 * m + 1, spot] = obuf[2 * m + 1, spot] + jnp.where(odd8, 0.0, corner)
+                else:
+                    DY[k, m] = DY[k, m] + corner
 
         if not ended:
             for m in (0, M - 1):
@@ -387,7 +423,6 @@
                     for t in tiles:
                         acc = pack(acc, t, value[8 * (t - tiles[0]):8 * (t - tiles[0]) + 8])
                 own[r + 1, m] = acc
-            start(r + 1, [q for q in edges if q[0]] + x_faces)
             for m in range(1, M - 1):
                 for t in (0, T - 1):
                     X[h + 2, m + 1, pl.ds(PAD + 8 * t, 8)] = black(m, [t])
@@ -395,20 +430,10 @@
                 high = jnp.where(group == T - 1, turn(DY[1, m], 4 * T - 2), 0.0)
                 own[r + 1, m] = (PK[m] + DZ[m]) + (low + high)
             finish_pack(r + 1)
-            start(r + 1, [q for q in ordered if not q[0]])
+            start(r + 1, ordered)
         else:
-            for m in range(M):
-                for tiles in chunks:
-                    begin, length = 8 * tiles[0], 8 * len(tiles)
-                    value = black(m, tiles)
-                    red = X[h + 1, m + 1, pl.ds(PAD + begin, length)] + spread(V[m + 1], tiles)
-                    extra = padded(tiles, DYR[0, m], DYR[1, m])
-                    if extra is not None:
-                        red = red + extra
-                    if m in (0, M - 1):
-                        red = red + DR[0 if m == 0 else 1, pl.ds(8 + begin, length)]
-                    obuf[2 * m, pl.ds(begin, length)] = jnp.where(odd_rows[:length], value, red)
-                    obuf[2 * m + 1, pl.ds(begin, length)] = jnp.where(odd_rows[:length], red, value)
+            finished(0)
+            finished(M - 1)
 
     for r in range(SWEEPS):
         for route in ROUTES:
@@ -437,7 +462,8 @@
             vmem(SWEEPS, 2, M, K),
             vmem(SWEEPS, 2, 2, M, K),
             vmem(M, 8, K),
-            vmem(2, M, 8, K),
+            vmem(2, -(-M // 4), 8, K),
+            vmem(2, -(-M // 4), 8, K),
             vmem(2, N // 2, K), vmem(2, N // 2, K),
             vmem(M, 8, K),
             vmem(M + 2, 8, K),
@@ -451,7 +477,7 @@
             vmem(2, M, 8, K),
             vmem(2, N + 16, K),
             vmem(2, N, K),
-            pltpu.SemaphoreType.DMA((2, 4)),
+            pltpu.SemaphoreType.DMA((7,)),
             pltpu.SemaphoreType.DMA((SWEEPS + 1, len(ROUTES))),
             pltpu.SemaphoreType.DMA((SWEEPS + 1, len(ROUTES))),
         ],

time: 31.7 us -> 30.9 us (0.975)
  Pallas kernels: 30.3 us -> 29.5 us
    pallas_call x1, Pallas kernels: 30.3 us -> 29.5 us  [on_device(): pl.pallas_call(kernel, out_shape=jax.ShapeDtypeStruct(field.shape, f32),...]
where the time goes in v3:
time: 30.9 us; the launch traced here: 30.8 us
  Pallas kernels  29.5 us (95%)
  local copies, waits for them, and re-layouts  1.32 us (4%)
    pallas_call x1, Pallas kernels, on_device(): pl.pallas_call(kernel, out_shape=jax.ShapeDtypeStruct(field.shape, f32),...  29.5 us
    unnamed x1, local copies, waits for them, and re-layouts  1.32 us

profile of v3, /device:TPU:1, one launch (start us, length us, event | category | flops | bytes accessed | tf_op | source)
XLA Modules:
  0.0 30.8 jit_solution(1987214642705331082)
XLA Ops:
  0.0 29.5 %shard_map.28 = f32[16,256,128]{2,1,0:T(8,128)S(1)} custom-call(f32[16,256,128]{2,1,0:T(8,128)} %field.1, f32[16,256,128]{2,1,0:T(8,128)} %source.1), custom_call_target="tpu_custom_call" | custom-call | tf_op jit(solution)/shard_map/pallas_call | solution.py:449
  29.5 1.3 %copy.4 = f32[16,256,128]{2,1,0:T(8,128)} copy(f32[16,256,128]{2,1,0:T(8,128)S(1)} %shard_map.28) | data formatting | bytes 4194304

commit v4 on v3

--- a/solution.py
+++ b/solution.py
@@ -106,6 +106,13 @@
         for route in routes:
             guarded(-route[0], lambda route=route: remote(r, route).wait_recv())
 
+    barrier = pltpu.get_barrier_semaphore()
+    count = jnp.int32(0)
+    for route in ordered:
+        guarded(route[0], lambda route=route: pl.semaphore_signal(
+            barrier, inc=1, device_id=target(route), device_id_type=MESH))
+        count = count + (1 if route[0] == 0 else has[side(route[0])].astype(jnp.int32))
+
     planes = 2 * M // 4
     spans = [(source, sbuf, 0, 2), (source, sbuf, 2 * M - 2, 2)]
     spans += [(field, fbuf, part * planes, planes) for part in range(4)]
@@ -116,13 +123,6 @@
     ]
     for load in loads:
         load.start()
-    barrier = pltpu.get_barrier_semaphore()
-    count = jnp.int32(0)
-    for route in ROUTES:
-        guarded(route[0], lambda route=route: pl.semaphore_signal(
-            barrier, inc=1, device_id=target(route), device_id_type=MESH))
-        count = count + (1 if route[0] == 0 else has[side(route[0])].astype(jnp.int32))
-
     lane = iota((8, LANES), 1)
     sub = iota((8, LANES), 0)
     group = lane // 4
@@ -381,22 +381,26 @@
                 half = sxin[k]
                 S[0, plane, pl.ds(PAD, N // 2)] = half
                 S[0, plane, pl.ds(PAD + N // 2, N // 2)] = pltpu.roll(half, LANES - 1, 1)
-        for k, (m, near) in enumerate(((-1, 0), (M, M - 1))):
+        for k, (plane, near) in enumerate(((0, 1), (M + 1, M))):
             for tiles in chunks:
-                begin, length = PAD + 8 * tiles[0], 8 * len(tiles)
+                length = 8 * len(tiles)
+                bare = X[h, plane, pl.ds(PAD + 8 * tiles[0], length)] * f32(SIXTH)
                 odd = odd_rows[:length]
-                red = update(h, m, begin, length, wings_of(U[k], tiles), near)
-                bare = X[h, m + 1, pl.ds(begin, length)] * f32(SIXTH)
-                if k == 0:
-                    red, bare = jnp.where(odd, red, 0.0), jnp.where(odd, 0.0, bare)
-                else:
-                    red, bare = jnp.where(odd, 0.0, red), jnp.where(odd, bare, 0.0)
-                DR[k, pl.ds(8 + 8 * tiles[0], length)] = bare
-                DX[k, pl.ds(8 * tiles[0], length)] = jnp.where(has[k], red, 0.0) + (bare + lane_sum(bare))
+                DR[k, pl.ds(8 + 8 * tiles[0], length)] = jnp.where(odd, bare, 0.0) if k else jnp.where(odd, 0.0, bare)
             for tiles in chunks:
                 begin, length = 8 * tiles[0], 8 * len(tiles)
-                here = pl.ds(begin, length)
-                DX[k, here] = (DX[k, here] + (DR[k, pl.ds(7 + begin, length)] + DR[k, pl.ds(9 + begin, length)])) * f32(SIXTH)
+                here, odd = pl.ds(PAD + begin, length), odd_rows[:length]
+                bare = DR[k, pl.ds(8 + begin, length)]
+                around = lane_sum(bare) + (DR[k, pl.ds(7 + begin, length)] + DR[k, pl.ds(9 + begin, length)])
+                rest = (S[0, plane, here] + X[h, plane, here]) + X[h, near, here]
+                rest = rest + jnp.where(outer_rows[:length], wings_of(U[k], tiles), 0.0)
+                if tiles[0] == 0:
+                    rest = rest + jnp.where(row_of[:length] == 0, X[h, plane, PAD - 1:PAD], 0.0)
+                if tiles[-1] == T - 1:
+                    rest = rest + jnp.where(row_of[:length] == length - 1, X[h, plane, PAD + N:PAD + N + 1], 0.0)
+                red = rest * f32(SIXTH) + around
+                red = jnp.where(odd, 0.0, red) if k else jnp.where(odd, red, 0.0)
+                DX[k, pl.ds(begin, length)] = (jnp.where(has[k], red, 0.0) + (bare + around)) * f32(SIXTH)
         wait(r, yz_edges)
         small = (M, LANES)
         spot = iota(small, 1) % 4

time: 30.9 us -> 30.7 us (level)
  no operation moved by 1% of the time
where the time goes in v4:
time: 30.7 us; the launch traced here: 30.6 us
  Pallas kernels  29.3 us (95%)
  local copies, waits for them, and re-layouts  1.32 us (4%)
    pallas_call x1, Pallas kernels, on_device(): pl.pallas_call(kernel, out_shape=jax.ShapeDtypeStruct(field.shape, f32),...  29.3 us
    unnamed x1, local copies, waits for them, and re-layouts  1.32 us

profile of v4, /device:TPU:1, one launch (start us, length us, event | category | flops | bytes accessed | tf_op | source)
XLA Modules:
  0.0 30.6 jit_solution(3313634335464674474)
XLA Ops:
  0.0 29.3 %shard_map.28 = f32[16,256,128]{2,1,0:T(8,128)S(1)} custom-call(f32[16,256,128]{2,1,0:T(8,128)} %field.1, f32[16,256,128]{2,1,0:T(8,128)} %source.1), custom_call_target="tpu_custom_call" | custom-call | tf_op jit(solution)/shard_map/pallas_call | solution.py:453
  29.3 1.3 %copy.4 = f32[16,256,128]{2,1,0:T(8,128)} copy(f32[16,256,128]{2,1,0:T(8,128)S(1)} %shard_map.28) | data formatting | bytes 4194304

commit v5 on v4

--- a/solution.py
+++ b/solution.py
@@ -12,7 +12,7 @@
 HALF = 2 * SWEEPS
 PAD = 16
 LANES = 128
-CHUNK = 8
+CHUNK = 16
 SIXTH = 1.0 / 6.0
 MESH = pl.DeviceIdType.MESH
 AXES = ("gx", "gy", "gz")
@@ -198,8 +198,6 @@
         value = split_source(m)
         top, bottom = value[:N // 2], pltpu.roll(value[N // 2:], 1, 1)
         sxout[k] = jnp.where(whole_odd[:N // 2], (bottom, top)[k], (top, bottom)[k])
-    pl.semaphore_wait(barrier, count)
-    start(SWEEPS, x_faces)
 
     for load in loads[2:6]:
         load.wait()
@@ -211,7 +209,9 @@
             acc = pack(acc, t, value[8 * t:8 * t + 8])
         own[0, m] = acc
     finish_pack(0)
+    pl.semaphore_wait(barrier, count)
     start(0, ordered)
+    start(SWEEPS, x_faces)
 
     for load in loads[6:]:
         load.wait()

time: 30.7 us -> 30.7 us (level)
  no operation moved by 1% of the time
where the time goes in v5:
time: 30.7 us; the launch traced here: 30.6 us
  Pallas kernels  29.3 us (95%)
  local copies, waits for them, and re-layouts  1.32 us (4%)
    pallas_call x1, Pallas kernels, on_device(): pl.pallas_call(kernel, out_shape=jax.ShapeDtypeStruct(field.shape, f32),...  29.3 us
    unnamed x1, local copies, waits for them, and re-layouts  1.32 us

profile of v5, /device:TPU:1, one launch (start us, length us, event | category | flops | bytes accessed | tf_op | source)
XLA Modules:
  0.0 30.6 jit_solution(8548398265639510201)
XLA Ops:
  0.0 29.3 %shard_map.28 = f32[16,256,128]{2,1,0:T(8,128)S(1)} custom-call(f32[16,256,128]{2,1,0:T(8,128)} %field.1, f32[16,256,128]{2,1,0:T(8,128)} %source.1), custom_call_target="tpu_custom_call" | custom-call | tf_op jit(solution)/shard_map/pallas_call | solution.py:453
  29.3 1.3 %copy.4 = f32[16,256,128]{2,1,0:T(8,128)} copy(f32[16,256,128]{2,1,0:T(8,128)S(1)} %shard_map.28) | data formatting | bytes 4194304
